TPU v7x, 32 devices: a whole 2x2x4 slice. The times are simulated.
32 devices in a mesh: dp: 8 (over y, x, core), tensor: 4 (over z).
Axes of the slice: x: 2, y: 2, z: 4, core: 2. Of those that a mesh axis runs over, the one named last changes fastest.
Arguments:
- acts: bfloat16 [8192, 3584], P('dp'), may hold values from -6 to 6
- cotangent: bfloat16 [8192, 18944], P('dp', 'tensor'), may hold values from -6 to 6
- hessian_ema: float32 [3584, 18944], P('dp', 'tensor'), may hold values from 0.02 to 2
- momentum: float32 [3584, 18944], P('dp', 'tensor'), may hold values from -0.12 to 0.12
- gamma_table: float32 [28], replicated, may hold values from 0.005 to 0.02
- layer_index: int32 [1], replicated, may hold values from 0 to 27
- step_count: int32 [1], replicated, may hold values from 1 to 20
Outputs:
- new_hessian: float32 [67895296], P(('dp', 'tensor'))
- ratio: float32 [67895296], P(('dp', 'tensor'))
All inputs are finite; a program needn't handle non-finite values.
Results may differ from a plain program's by a relative error of at most 0.0003.
Values sent between devices are 32-bit elements; how exact they have to be, the bound alone decides.
No kernel may reach another device: no remote copies, remote signals or barrier semaphores. Data moves between devices by JAX's collectives and lax.ppermute only.
A program may use at most 192 MiB of HBM per device.

v0:
```python
import jax
import jax.numpy as jnp
from jax import lax
from jax.sharding import PartitionSpec as P


def settle(grad_part, hess_part, mom_part, tokens_all, gamma, correction):
    estimate = grad_part * grad_part / tokens_all
    fresh = 0.99 * hess_part + 0.01 * estimate
    corrected = fresh / correction
    ratio = jnp.clip(mom_part / (gamma * corrected), -1.0, 1.0)
    return (fresh, ratio)


def on_device(acts, cotangent, hessian_ema, momentum, gamma_table, layer_index, step_count):
    tokens_all = float(acts.shape[0] * lax.axis_size("dp"))
    picks = jnp.arange(gamma_table.shape[0], dtype=jnp.int32) == layer_index[0]
    gamma = jnp.sum(jnp.where(picks, gamma_table, jnp.zeros_like(gamma_table)))
    correction = 1.0 - jnp.power(
        jnp.asarray(0.99, gamma_table.dtype), step_count[0].astype(gamma_table.dtype)
    )
    grad_rows = lax.psum_scatter(
        lax.dot_general(
            acts, cotangent, (((0,), (0,)), ((), ())), preferred_element_type=jnp.float32
        ),
        "dp",
        scatter_dimension=0,
        tiled=True,
    )
    moved_grad, moved_hess, moved_mom = (
        lax.all_to_all(grad_rows, "tensor", split_axis=0, concat_axis=1, tiled=True),
        lax.all_to_all(hessian_ema, "tensor", split_axis=0, concat_axis=1, tiled=True),
        lax.all_to_all(momentum, "tensor", split_axis=0, concat_axis=1, tiled=True),
    )
    fresh, ratio = settle(moved_grad, moved_hess, moved_mom, tokens_all, gamma, correction)
    return (fresh.reshape(-1), ratio.reshape(-1))


def solution(mesh):
    placed = (P("dp", None), P("dp", "tensor"), P("dp", "tensor"), P("dp", "tensor"), P(), P(), P())
    return jax.shard_map(
        on_device,
        mesh=mesh,
        in_specs=placed,
        out_specs=(P(("dp", "tensor")), P(("dp", "tensor"))),
        check_vma=False,
    )
```

profile of v0, /device:TPU:0, one launch (start us, length us, event | category | flops | bytes accessed | tf_op | source)
XLA Modules:
  0.0 698.3 jit_solution(11572785254212841880)
XLA Ops:
  7.2 0.0 reduce-scatter.2.cloned.1.call-start
  7.2 45.5 %fusion.1 = f32[3584,4736]{1,0:T(8,128)} fusion(bf16[1024,3584]{1,0:T(8,128)(2,1)} %param.7, bf16[1024,4736]{1,0:T(8,128)(2,1)} %param.8), kind=kOutput, calls=%fused_computation.4 | convolution fusion | flops 34762391552 | bytes 84934656 | tf_op jit(solution)/shard_map/dot_general | solution.py:23
  52.7 0.0 reduce-scatter.2.cloned.1.call-update
  52.7 0.0 copy-start
  52.7 195.0 %all_to_all.45 = f32[4,112,4736]{2,1,0:T(8,128)} all-to-all(f32[4,112,4736]{2,1,0:T(8,128)} %bitcast.12), channel_id=1, replica_groups=mesh['dp'=8,'tensor'=4] {'tensor'}, dimensions={0} | all-to-all | bytes 16973824 | tf_op jit(solution)/shard_map/all_to_all | solution.py:32
  247.7 0.0 copy-done
  247.7 188.6 %all_to_all.46 = f32[4,112,4736]{2,1,0:T(8,128)} all-to-all(f32[4,112,4736]{2,1,0:T(8,128)S(1)} %bitcast.13), channel_id=1, replica_groups=mesh['dp'=8,'tensor'=4] {'tensor'}, dimensions={0} | all-to-all | bytes 16973824 | tf_op jit(solution)/shard_map/all_to_all | solution.py:33
  436.3 22.5 %reduce-scatter.2.cloned.1.call-done = f32[448,4736]{1,0:T(8,128)} async-done(((f32[3584,4736]{1,0:T(8,128)}), f32[448,4736]{1,0:T(8,128)}) %reduce-scatter.2.cloned.1.call-update) | async-done | bytes 8486928 | tf_op jit(solution)/shard_map/reduce_scatter | solution.py:22
  458.9 0.0 copy-start.1
  458.9 6.0 all-to-all-start.1
  466.2 0.0 copy-done.1
  466.2 0.6 fusion
  466.8 10.1 %copy.13 = f32[112,4,4736]{2,1,0:T(4,128)} copy(f32[112,4,4736]{2,0,1:T(8,128)} %bitcast.11) | data formatting | bytes 16973824 | tf_op jit(solution)/shard_map/all_to_all | solution.py:33
  476.9 10.4 %all_to_all.41 = f32[2121728]{0:T(1024)} reshape(f32[112,4,4736]{2,1,0:T(4,128)} %copy.13) | data formatting | bytes 16973824 | tf_op jit(solution)/shard_map/all_to_all | solution.py:33
  487.3 162.7 %all-to-all-done.1 = f32[4,112,4736]{2,1,0:T(8,128)} async-done(((f32[4,112,4736]{2,1,0:T(8,128)}), f32[4,112,4736]{2,1,0:T(8,128)}, u32[]{:S(2)}, u32[]{:S(2)}) %all-to-all-start.1) | async-done | bytes 8486944 | tf_op jit(solution)/shard_map/all_to_all | solution.py:31
  650.0 10.5 %add_bitcast_fusion = f32[112,4,4736]{2,0,1:T(8,128)} fusion(f32[4,112,4736]{2,1,0:T(8,128)} %all-to-all-done.1, f32[4,112,4736]{2,1,0:T(8,128)} %all_to_all.45), kind=kLoop, calls=%fused_computation.1 | loop fusion | flops 8486912 | bytes 25460736 | tf_op jit(solution)/shard_map/add | solution.py:9
  660.5 9.9 %copy.12 = f32[112,4,4736]{2,1,0:T(4,128)} copy(f32[112,4,4736]{2,0,1:T(8,128)} %add_bitcast_fusion) | data formatting | bytes 16973824 | tf_op jit(solution)/shard_map/add | solution.py:9
  670.5 10.3 %add.15 = f32[2121728]{0:T(1024)} reshape(f32[112,4,4736]{2,1,0:T(4,128)} %copy.12) | data formatting | bytes 16973824 | tf_op jit(solution)/shard_map/add | solution.py:9
  680.8 10.7 %divide_clamp_fusion = f32[2121728]{0:T(1024)} fusion(f32[2121728]{0:T(1024)} %all_to_all.41, f32[2121728]{0:T(1024)} %add.15, f32[]{:T(128)} %bitcast.6, f32[]{:T(128)} %fusion), kind=kLoop, calls=%fused_computation | loop fusion | flops 8486912 | bytes 25460744 | tf_op jit(solution)/shard_map/jit(clip)/min | solution.py:11
Async XLA Ops:
  7.2 451.7 %reduce-scatter.2.cloned.1.call-start = ((), (), s32[]{:S(2)}) async-start(), calls=%async_computation.4 | async-start | bytes 76382208 | tf_op jit(solution)/shard_map/reduce_scatter | solution.py:22
  52.7 195.0 %copy-start = (f32[448,4736]{1,0:T(8,128)S(1)}, f32[448,4736]{1,0:T(8,128)}, u32[]{:S(2)}) copy-start(f32[448,4736]{1,0:T(8,128)} %param.10) | copy-start | bytes 25460740
  458.9 7.3 %copy-start.1 = (f32[28]{0:T(128)S(1)}, f32[28]{0:T(128)}, u32[]{:S(2)}) copy-start(f32[28]{0:T(128)} %param.11) | copy-start | bytes 340
  458.9 191.1 %all-to-all-start.1 = ((f32[4,112,4736]{2,1,0:T(8,128)}), f32[4,112,4736]{2,1,0:T(8,128)}, u32[]{:S(2)}, u32[]{:S(2)}) async-start(f32[4,112,4736]{2,1,0:T(8,128)} %bitcast.14), calls=%async_computation.2 | async-start | bytes 16973824 | tf_op jit(solution)/shard_map/all_to_all | solution.py:31
Sparse Core Ops, SparseCore 0:
  52.8 405.9 reduce-scatter.1
where the time goes:
time: 699 us; the launch traced here: 698 us
  blocking collectives  384 us (55%)
  waiting for transfers between devices  185 us (26%)
  matrix products  45.5 us (7%)
  local copies, waits for them, and re-layouts  40.8 us (6%)
  other arithmetic  21.8 us (3%)
  between operations  15.4 us (2%)
    all_to_all x1, blocking collectives, on_device(): lax.all_to_all(hessian_ema, 'tensor', split_axis=0, concat_axis=1, tiled=...  195 us
    all_to_all x1, blocking collectives, on_device(): lax.all_to_all(momentum, 'tensor', split_axis=0, concat_axis=1, tiled=True)  189 us
    all_to_all x1, waiting for transfers between devices, on_device(): lax.all_to_all(grad_rows, 'tensor', split_axis=0, concat_axis=1, tiled=True)  163 us
    dot_general x1, matrix products, on_device(): lax.dot_general(acts, cotangent, (((0,), (0,)), ((), ())), preferred_elem...  45.5 us
    reduce_scatter x1, waiting for transfers between devices, on_device(): lax.psum_scatter(lax.dot_general(acts, cotangent, (((0,), (0,)), ((), ())...  22.5 us
    all_to_all x2, local copies, waits for them, and re-layouts, on_device(): lax.all_to_all(momentum, 'tensor', split_axis=0, concat_axis=1, tiled=True)  20.5 us
    add x2, local copies, waits for them, and re-layouts, settle(): fresh = 0.99 * hess_part + 0.01 * estimate  20.3 us
  transfers between devices with their start and end apart: 2, of which 2 were waited for; matrix products, arithmetic and copies ran while one was open for 2% of the time, Pallas kernels for 0%

commit v1 on v0

v1 whole, which is shorter than its diff:
```python
import jax
import jax.numpy as jnp
from jax import lax
from jax.experimental import pallas as pl
from jax.experimental.pallas import tpu as pltpu
from jax.sharding import PartitionSpec as P

LANES = 128
SUBLANES = 8
WRITE_LAG = 2


def row_chunks(rows):
    step = 16
    if rows % step:
        return [rows]
    count = rows // step
    double = count // 3
    return [2 * step] * double + [step] * (count - 2 * double)


def flat_kernel(where, scal, *refs, tp, per_row):
    fresh_in = refs[:tp]
    mom_in = refs[tp : 2 * tp]
    fresh_out, ratio_out = refs[-2:]
    gamma = scal[0]
    correction = scal[1]
    for s in range(tp):
        base = where[s] * per_row
        for j in range(per_row):
            cols = slice(j * LANES, (j + 1) * LANES)
            fresh = fresh_in[s][:, cols]
            ratio = jnp.clip(mom_in[s][:, cols] / (gamma * (fresh / correction)), -1.0, 1.0)
            rows = pl.ds(base + j, SUBLANES, stride=tp * per_row)
            fresh_out[rows, :] = fresh
            ratio_out[rows, :] = ratio


def write_flat(where, scal, fresh, mom, first, rows, outs):
    tp = len(fresh)
    n, cols = fresh[0].shape
    per_row = cols // LANES
    step0 = first // SUBLANES
    own_step = rows // SUBLANES
    in_specs = [pl.BlockSpec((SUBLANES, cols), lambda i, *_: (i, 0)) for _ in range(tp)]
    in_specs.append(pl.BlockSpec((SUBLANES, cols), lambda i, where, scal: (where[0] * own_step + step0 + i, 0)))
    in_specs += [pl.BlockSpec((SUBLANES, cols), lambda i, *_: (step0 + i, 0)) for _ in range(tp - 1)]
    block = (SUBLANES * tp * per_row, LANES)
    out_specs = [pl.BlockSpec(block, lambda i, *_: (step0 + i, 0)) for _ in range(2)]
    shape = jax.ShapeDtypeStruct((rows * tp * per_row, LANES), jnp.float32)
    aliases = {}
    if outs is not None:
        in_specs += [pl.BlockSpec(memory_space=pl.ANY)] * 2
        aliases = {2 + 2 * tp: 0, 3 + 2 * tp: 1}

    def body(where, scal, *refs):
        flat_kernel(where, scal, *refs, tp=tp, per_row=per_row)

    return pl.pallas_call(
        body,
        grid_spec=pltpu.PrefetchScalarGridSpec(
            num_scalar_prefetch=2,
            grid=(n // SUBLANES,),
            in_specs=in_specs,
            out_specs=out_specs,
        ),
        out_shape=(shape, shape),
        input_output_aliases=aliases,
        compiler_params=pltpu.CompilerParams(dimension_semantics=("arbitrary",)),
        name="write_flat",
    )(where, scal, *fresh, *mom, *(outs or ()))


def turn_kernel(where, acts_ref, *refs, chunks, dp, tp, rows):
    outs, scratch = refs[:-1], refs[-1]
    step = pl.program_id(0)
    width = acts_ref.shape[1]
    scratch[pl.ds(pl.multiple_of(step * width, width), width), :] = acts_ref[...].T

    @pl.when(step == pl.num_programs(0) - 1)
    def _():
        first = 0
        for k, n in enumerate(chunks):
            for core in range(2):
                for delta in range(dp // 2):
                    for s in range(tp):
                        row = where[(2 * delta + 1 - core) * tp + s] * rows + first
                        at = (delta * tp + s) * n
                        outs[2 * k + core][at : at + n, :] = scratch[pl.ds(pl.multiple_of(row, 16), n), :]
            first += n


def acts_by_chunk(acts, me, at, dp, tp, chunks):
    tokens, width = acts.shape
    rows = width // (dp * tp)
    deltas = me ^ jnp.arange(dp, dtype=jnp.int32)
    turns = (at + jnp.arange(tp, dtype=jnp.int32)) % tp
    order = (deltas[:, None] * tp + turns[None, :]).reshape(-1)
    wide = 512
    if rows % 16 or width % wide:
        whole = jnp.take(acts.T.reshape(dp * tp, rows, tokens), order, axis=0, mode="clip")
        whole = whole.reshape(dp // 2, 2, tp, rows, tokens)
        out, first = [], 0
        for n in chunks:
            for core in (1, 0):
                out.append(whole[:, core, :, first : first + n].reshape(-1, tokens))
            first += n
        return out

    def body(where, acts_ref, *refs):
        turn_kernel(where, acts_ref, *refs, chunks=chunks, dp=dp, tp=tp, rows=rows)

    shapes = [jax.ShapeDtypeStruct((dp // 2 * tp * n, tokens), acts.dtype) for n in chunks for _ in range(2)]
    return pl.pallas_call(
        body,
        grid_spec=pltpu.PrefetchScalarGridSpec(
            num_scalar_prefetch=1,
            grid=(width // wide,),
            in_specs=[pl.BlockSpec((tokens, wide), lambda i, *_: (0, i))],
            out_specs=[pl.BlockSpec(s.shape, lambda i, *_: (0, 0)) for s in shapes],
            scratch_shapes=[pltpu.VMEM((width, tokens), acts.dtype)],
        ),
        out_shape=shapes,
        compiler_params=pltpu.CompilerParams(dimension_semantics=("arbitrary",), vmem_limit_bytes=48 * 1024 * 1024),
        name="acts_turn",
    )(order, acts)


def after(x, dep):
    return lax.optimization_barrier((x, dep))[0]


def product(lhs, rhs):
    return lax.dot_general(lhs, rhs, (((1,), (0,)), ((), ())), preferred_element_type=jnp.float32)


def on_device(acts, cotangent, hessian_ema, momentum, gamma_table, layer_index, step_count, dp, tp):
    tokens, width = acts.shape
    cols = cotangent.shape[1]
    tokens_all = float(tokens * dp)
    rows = width // (dp * tp)
    picks = jnp.arange(gamma_table.shape[0], dtype=jnp.int32) == layer_index[0]
    gamma = jnp.sum(jnp.where(picks, gamma_table, jnp.zeros_like(gamma_table)))
    correction = 1.0 - jnp.power(
        jnp.asarray(0.99, gamma_table.dtype), step_count[0].astype(gamma_table.dtype)
    )
    me = lax.axis_index("dp")
    at = lax.axis_index("tensor")
    bits = dp.bit_length() - 1

    def turn(x, s):
        return lax.ppermute(x, "tensor", [(i, (i + s) % tp) for i in range(tp)])

    def swap(x, b):
        return lax.ppermute(x, "dp", [(i, i ^ (1 << b)) for i in range(dp)])

    hess = hessian_ema.reshape(tp, rows, cols)
    mom = momentum.reshape(tp, rows, cols)

    def block(x, s):
        return lax.dynamic_index_in_dim(x, (at + s) % tp, 0, keepdims=False)

    mom_moved, source = [], mom
    for s in range(1, tp):
        sent = block(source, s)
        mom_moved.append(turn(sent, s))
        source = after(mom, sent)

    chunks = row_chunks(rows)
    lhs = acts_by_chunk(acts, me, at, dp, tp, chunks)

    where = (at - jnp.arange(tp, dtype=jnp.int32)) % tp
    scal = jnp.stack([gamma, correction])
    aligned = cols % LANES == 0 and rows % SUBLANES == 0
    halves = 2 if tp % 2 == 0 else 1
    firsts = [sum(chunks[:k]) for k in range(len(chunks))]
    stages = max(bits - 1, 1)

    def send_dot(k, dep):
        part = product(after(lhs[2 * k], dep), cotangent)
        return part, swap(part, 0)

    def own_dot(k, moved, dep):
        chip = product(after(lhs[2 * k + 1], dep), cotangent) + moved
        blocks = chip.reshape((2,) * (bits - 1) + (tp, chunks[k], cols))
        parts = []
        for h in range(halves):
            axes = list(range(1, bits))
            if h:
                axes.reverse()
            half = blocks[..., h * tp // halves : (h + 1) * tp // halves, :, :]
            parts.append(([half], axes, list(range(bits - 1, 0, -1))))
        return chip, parts

    def exchange(parts, stage, dep):
        out = []
        for terms, axes, left in parts:
            b = axes[stage]
            pos = left.index(b)
            sides = [lax.index_in_dim(x, 1, pos, keepdims=False) for x in terms]
            sides[0] = after(sides[0], dep)
            send = sum(sides[1:], sides[0])
            dep = send
            moved = swap(send, b)
            keep = [lax.index_in_dim(x, 0, pos, keepdims=False) for x in terms]
            out.append((keep + [moved], axes, [x for x in left if x != b]))
        return out, dep

    def fresh_of(k, parts, dep):
        own = slice(firsts[k], firsts[k] + chunks[k])
        source = after(hess, dep)
        out = []
        for s in range(tp):
            terms = [x[s % (tp // halves)] for x in parts[s * halves // tp][0]]
            grad = sum(terms[1:], terms[0])
            estimate = grad * grad / tokens_all
            out.append(0.99 * block(source[:, own], s) + 0.01 * estimate)
        moved = [out[0]]
        for s in range(1, tp):
            moved.append(turn(out[s], s))
        return moved, out[-1]

    def write(k, outs, dep):
        return write_flat(where, after(scal, dep), fresh[k], [momentum, *mom_moved], firsts[k], rows, outs)

    count = len(chunks)
    pairs, parts, fresh, outs = {}, {}, {}, None
    dep = lhs[0]
    for k in range(min(2, count)):
        dep, pairs[k] = send_dot(k, dep)
    for step in range(count + stages):
        if step < count:
            dep, parts[step] = own_dot(step, pairs[step], dep)
        for stage in range(stages):
            j = step - stage
            if 0 <= j < count:
                parts[j], dep = exchange(parts[j], stage, dep)
        j = step - stages
        if 0 <= j < count:
            if aligned and j >= WRITE_LAG:
                outs = write(j - WRITE_LAG, outs, dep)
                dep = outs[0]
            fresh[j], dep = fresh_of(j, parts[j], dep)
        if step + 2 < count:
            dep, pairs[step + 2] = send_dot(step + 2, dep)
    if aligned:
        for j in range(max(count - WRITE_LAG, 0), count):
            outs = write(j, outs, dep)
    pieces = [fresh[k] for k in range(count)]
    if aligned:
        return tuple(o.reshape(-1) for o in outs)
    fresh = [jnp.concatenate([p[s] for p in pieces], axis=0) for s in range(tp)]
    moms = [block(mom, 0), *mom_moved]

    def in_order(parts):
        stacked = jnp.stack(parts)
        return jnp.concatenate([lax.dynamic_index_in_dim(stacked, (at - i) % tp, 0, keepdims=False) for i in range(tp)], axis=1)

    fresh_rows = in_order(fresh)
    ratio = jnp.clip(in_order(moms) / (gamma * (fresh_rows / correction)), -1.0, 1.0)
    return fresh_rows.reshape(-1), ratio.reshape(-1)


def solution(mesh):
    dp, tp = mesh.shape["dp"], mesh.shape["tensor"]
    placed = (P("dp", None), P("dp", "tensor"), P("dp", "tensor"), P("dp", "tensor"), P(), P(), P())

    def body(*args):
        return on_device(*args, dp=dp, tp=tp)

    return jax.shard_map(
        body,
        mesh=mesh,
        in_specs=placed,
        out_specs=(P(("dp", "tensor")), P(("dp", "tensor"))),
        check_vma=False,
    )
```

time: 699 us -> 536 us (0.77)
  blocking collectives: 384 us -> 0 us
  waiting for transfers between devices: 185 us -> 298 us
  starting transfers between devices: 6.03 us -> 58.9 us
  Pallas kernels: 0 us -> 31.4 us
  matrix products: 45.5 us -> 67 us
  other arithmetic: 21.8 us -> 37.8 us
  between operations: 15.4 us -> 2.44 us
    all_to_all x2 -> x0, blocking collectives: 384 us -> none  [the longest x1 195 us: on_device(): lax.all_to_all(hessian_ema, 'tensor', split_axis=0, concat_axis=1, tiled=...]
    ppermute x0 -> x43, waiting for transfers between devices: none -> 298 us  [the longest x25 168 us: swap(): return lax.ppermute(x, 'dp', [(i, i ^ 1 << b) for i in range(dp)])]
    all_to_all x1 -> x0, waiting for transfers between devices: 163 us -> none  [on_device(): lax.all_to_all(grad_rows, 'tensor', split_axis=0, concat_axis=1, tiled=True)]
    ppermute x0 -> x43, starting transfers between devices: none -> 58.9 us  [the longest x18 33.4 us: turn(): return lax.ppermute(x, 'tensor', [(i, (i + s) % tp) for i in range(tp)])]
    pallas_call x0 -> x6, Pallas kernels: none -> 31.4 us  [the longest x5 22.4 us: write_flat(): pl.pallas_call(body, grid_spec=pltpu.PrefetchScalarGridSpec(num_scalar_pr...]
    squeeze x0 -> x18, local copies, waits for them, and re-layouts: none -> 26.8 us  [the longest x15 17.4 us: exchange(): sides = [lax.index_in_dim(x, 1, pos, keepdims=False) for x in terms]]
    add x1 -> x16, other arithmetic: 10.5 us -> 35.4 us  [the longest x5 17.7 us: fresh_of(): out.append(0.99 * block(source[:, own], s) + 0.01 * estimate)]
    reduce_scatter x1 -> x0, waiting for transfers between devices: 22.5 us -> none  [on_device(): lax.psum_scatter(lax.dot_general(acts, cotangent, (((0,), (0,)), ((), ())...]
  transfers between devices with their start and end apart: 2 -> 43, of which waited for: 2 -> 15; matrix products, arithmetic and copies ran while one was open for 2% -> 24% of each run, Pallas kernels for 0% -> 4%
where the time goes in v1:
time: 536 us; the launch traced here: 535 us
  waiting for transfers between devices  298 us (56%)
  matrix products  67 us (12%)
  starting transfers between devices  58.9 us (11%)
  local copies, waits for them, and re-layouts  39.5 us (7%)
  other arithmetic  37.8 us (7%)
  Pallas kernels  31.4 us (6%)
    ppermute x25, waiting for transfers between devices, swap(): return lax.ppermute(x, 'dp', [(i, i ^ 1 << b) for i in range(dp)])  168 us
    ppermute x18, waiting for transfers between devices, turn(): return lax.ppermute(x, 'tensor', [(i, (i + s) % tp) for i in range(tp)])  129 us
    dot_general x10, matrix products, product(): lax.dot_general(lhs, rhs, (((1,), (0,)), ((), ())), preferred_element_typ...  67 us
    ppermute x18, starting transfers between devices, turn(): return lax.ppermute(x, 'tensor', [(i, (i + s) % tp) for i in range(tp)])  33.4 us
    ppermute x25, starting transfers between devices, swap(): return lax.ppermute(x, 'dp', [(i, i ^ 1 << b) for i in range(dp)])  25.5 us
    pallas_call x5, Pallas kernels, write_flat(): pl.pallas_call(body, grid_spec=pltpu.PrefetchScalarGridSpec(num_scalar_pr...  22.4 us
    add x5, other arithmetic, fresh_of(): out.append(0.99 * block(source[:, own], s) + 0.01 * estimate)  17.7 us
    add x10, other arithmetic, exchange(): send = sum(sides[1:], sides[0])  17.6 us
  transfers between devices with their start and end apart: 43, of which 15 were waited for; matrix products, arithmetic and copies ran while one was open for 24% of the time, Pallas kernels for 4%

profile of v1, /device:TPU:0, one launch (start us, length us, event | category | flops | bytes accessed | tf_op | source)
XLA Modules:
  0.0 534.8 jit_solution(6096756492888787864)
XLA Ops:
  0.8 9.0 %acts_turn.1 = (bf16[512,1024]{1,0:T(8,128)(2,1)S(1)}, bf16[512,1024]{1,0:T(8,128)(2,1)S(1)}, bf16[512,1024]{1,0:T(8,128)(2,1)}, bf16[512,1024]{1,0:T(8,128)(2,1...) custom-call(s32[32]{0:T(128)S(1)} %add.360.where, ...), custom_call_target="tpu_custom_call" | custom-call | tf_op jit(solution)/shard_map/acts_turn/pallas_call | solution.py:114
  9.8 12.0 %fusion.113 = f32[512,4736]{1,0:T(8,128)} fusion(bf16[512,1024]{1,0:T(8,128)(2,1)S(1)} %get-tuple-element.67, bf16[1024,4736]{1,0:T(8,128)(2,1)} %param.8), kind=kOutput, calls=%fused_computation.221 | convolution fusion | flops 4966055936 | bytes 20447232 | tf_op jit(solution)/shard_map/dot_general | solution.py:134
  22.3 7.8 %fusion.114 = f32[512,4736]{1,0:T(8,128)} fusion(bf16[512,1024]{1,0:T(8,128)(2,1)S(1)} %copy-done.34, bf16[1024,4736]{1,0:T(8,128)(2,1)S(1)} %bitcast.565), kind=kOutput, calls=%fused_computation.222 | convolution fusion | flops 4966055936 | bytes 20447232 | tf_op jit(solution)/shard_map/dot_general | solution.py:134
  30.2 3.1 dynamic-slice_bitcast_fusion.2
  33.3 3.1 dynamic-slice_bitcast_fusion.1
  36.3 4.0 collective-permute-start.20
  44.1 3.2 dynamic-slice_bitcast_fusion
  47.3 10.9 %convolution_add_fusion.1 = f32[512,4736]{1,0:T(8,128)S(1)} fusion(f32[512,4736]{1,0:T(8,128)} %collective-permute-done, bf16[512,1024]{1,0:T(8,128)(2,1)S(1)} %get-tuple-element.69, bf16[1024,4736]{1,0:T(8,128)(2,1)} %param.8), kind=kOutput, calls=%fused_computation.1 | convolution fusion | flops 4968480768 | bytes 30146560 | tf_op jit(solution)/shard_map/dot_general | solution.py:134
  58.3 1.6 slice_bitcast_fusion.2
  61.4 2.2 slice_bitcast_fusion.3
  63.6 1.5 collective-permute-start.3
  65.1 4.4 fusion.115
  71.1 8.1 %convolution_add_fusion = f32[512,4736]{1,0:T(8,128)S(1)} fusion(f32[512,4736]{1,0:T(8,128)} %collective-permute-done.1, bf16[512,1024]{1,0:T(8,128)(2,1)S(1)} %copy-done.20, bf16[1024,4736]{1,0:T(8,128)(2,1)S(1)} %bitcast.567), kind=kOutput, calls=%fused_computation | convolution fusion | flops 4968480768 | bytes 30146560 | tf_op jit(solution)/shard_map/dot_general | solution.py:134
  79.1 1.7 slice_bitcast_fusion
  80.9 1.6 slice_bitcast_fusion.1
  83.2 31.3 %collective-permute-done.2 = f32[2,2,32,4736]{3,2,1,0:T(8,128)} collective-permute-done((f32[2,2,32,4736]{3,2,1,0:T(8,128)}, f32[2,2,32,4736]{3,2,1,0:T(8,128)}, u32[]{:S(2)}, u32[]{:S(2)}) %collective-permute-start.2) | collective-permute-done | bytes 2424864 | tf_op jit(solution)/shard_map/ppermute | solution.py:155
  116.0 2.5 fusion.3
  119.4 2.4 fusion.2
  121.8 4.4 fusion.116
  127.8 5.0 convolution_add_fusion.4
  134.0 1.6 slice_bitcast_fusion.11
  135.6 34.7 %collective-permute-done.5 = f32[2,2,32,4736]{3,2,1,0:T(8,128)} collective-permute-done((f32[2,2,32,4736]{3,2,1,0:T(8,128)}, f32[2,2,32,4736]{3,2,1,0:T(8,128)}, u32[]{:S(2)}, u32[]{:S(2)}) %collective-permute-start.5) | collective-permute-done | bytes 2424864 | tf_op jit(solution)/shard_map/ppermute | solution.py:155
  170.4 2.6 fusion.1
  172.9 2.5 fusion
  176.9 1.9 slice.496
  178.8 17.5 %collective-permute-done.7 = f32[2,32,4736]{2,1,0:T(8,128)S(1)} collective-permute-done((f32[2,32,4736]{2,1,0:T(8,128)}, f32[2,32,4736]{2,1,0:T(8,128)S(1)}, u32[]{:S(2)}, u32[]{:S(2)}) %collective-permute-start.7) | collective-permute-done | bytes 1212448 | tf_op jit(solution)/shard_map/ppermute | solution.py:155
  199.2 4.3 fusion.24
  203.5 4.4 fusion.117
  208.1 5.0 convolution_add_fusion.3
  215.4 30.9 %collective-permute-done.9 = f32[2,2,16,4736]{3,2,1,0:T(8,128)} collective-permute-done((f32[2,2,16,4736]{3,2,1,0:T(8,128)}, f32[2,2,16,4736]{3,2,1,0:T(8,128)}, u32[]{:S(2)}, u32[]{:S(2)}) %collective-permute-start.9) | collective-permute-done | bytes 1212448 | tf_op jit(solution)/shard_map/ppermute | solution.py:155
  246.2 1.5 collective-permute-start.25
  247.8 2.0 fusion.44
  249.7 1.6 collective-permute-start.19
  251.3 2.0 fusion.43
  253.3 3.3 slice.504
  256.6 2.2 collective-permute-start.21
  258.8 14.1 %collective-permute-done.25 = f32[2,32,4736]{2,1,0:T(8,128)} collective-permute-done((f32[2,32,4736]{2,1,0:T(8,128)S(1)}, f32[2,32,4736]{2,1,0:T(8,128)}, u32[]{:S(2)}, u32[]{:S(2)}) %collective-permute-start.25) | collective-permute-done | bytes 1212448 | tf_op jit(solution)/shard_map/ppermute | solution.py:155
  274.5 4.7 fusion.7
  279.3 1.6 collective-permute-start.13
  280.9 5.0 convolution_add_fusion.2
  288.2 16.9 %collective-permute-done.13 = f32[2,2,16,4736]{3,2,1,0:T(8,128)S(1)} collective-permute-done((f32[2,2,16,4736]{3,2,1,0:T(8,128)}, f32[2,2,16,4736]{3,2,1,0:T(8,128)S(1)}, u32[]{:S(2)}, u32[]{:S(2)}) %collective-permute-start.13) | collective-permute-done | bytes 1212448 | tf_op jit(solution)/shard_map/ppermute | solution.py:155
  307.4 36.3 %collective-permute-done.21.refs_7_ = f32[112,4736]{1,0:T(8,128)S(1)} collective-permute-done((f32[112,4736]{1,0:T(8,128)}, f32[112,4736]{1,0:T(8,128)S(1)}, u32[]{:S(2)}, u32[]{:S(2)}) %collective-permute-start.21) | collective-permute-done | bytes 2121760 | tf_op jit(solution)/shard_map/ppermute | solution.py:152
  343.7 3.2 collective-permute-start.17
  346.9 1.6 collective-permute-start.16
  348.5 1.6 collective-permute-start.22
  351.6 43.5 %collective-permute-done.17.refs_2_ = f32[32,4736]{1,0:T(8,128)S(1)} collective-permute-done((f32[32,4736]{1,0:T(8,128)S(1)}, f32[32,4736]{1,0:T(8,128)S(1)}, u32[]{:S(2)}, u32[]{:S(2)}) %collective-permute-start.17) | collective-permute-done | bytes 606240 | tf_op jit(solution)/shard_map/ppermute | solution.py:152
  398.0 5.8 %write_flat.5 = (f32[16576,128]{1,0:T(8,128)}, f32[16576,128]{1,0:T(8,128)}) custom-call(s32[4]{0:T(128)} %and_select_fusion.1.where, f32[2]{0:T(128)} %pad_maximum_fusion.scal, f32[32,4736]{1,0:T(8,128)} %get-tuple-element.132.refs_0_, f32[32,4736]{1,0:T(8,128)} %copy-done.27, f32[32,4736]{1,0:T(8,128)} %copy-done.26, f32[32,4736]{1,0:T(8,128)} %copy-done.25, ...), custom_call_target="tpu_custom_call" | custom-call | tf_op jit(solution)/shard_map/write_flat/pallas_call | solution.py:59
  407.2 3.1 fusion.88
  411.6 22.0 %collective-permute-done.23 = f32[2,2,16,4736]{3,2,1,0:T(8,128)S(1)} collective-permute-done((f32[2,2,16,4736]{3,2,1,0:T(8,128)}, f32[2,2,16,4736]{3,2,1,0:T(8,128)S(1)}, u32[]{:S(2)}, u32[]{:S(2)}) %collective-permute-start.23) | collective-permute-done | bytes 1212448 | tf_op jit(solution)/shard_map/ppermute | solution.py:155
  438.5 9.0 %collective-permute-done.27.refs_2_ = f32[32,4736]{1,0:T(8,128)} collective-permute-done((f32[32,4736]{1,0:T(8,128)}, f32[32,4736]{1,0:T(8,128)}, u32[]{:S(2)}, u32[]{:S(2)}) %collective-permute-start.27) | collective-permute-done | bytes 606240 | tf_op jit(solution)/shard_map/ppermute | solution.py:152
  447.5 3.4 collective-permute-start.32
  451.0 5.9 %write_flat.6 = (f32[16576,128]{1,0:T(8,128)}, f32[16576,128]{1,0:T(8,128)}) custom-call(s32[4]{0:T(128)} %and_select_fusion.1.where, f32[2]{0:T(128)} %pad_maximum_fusion.scal, f32[32,4736]{1,0:T(8,128)} %get-tuple-element.130.refs_0_, f32[32,4736]{1,0:T(8,128)} %collective-permute-done.26.refs_1_, ...), custom_call_target="tpu_custom_call", output_to_operand_aliasing={{0}: (10, {}), {1}: (11, {})} | custom-call | tf_op jit(solution)/shard_map/write_flat/pallas_call | solution.py:59
  458.3 1.6 collective-permute-start.34
  460.4 2.9 fusion.53
  463.2 10.9 %collective-permute-done.32.refs_2_ = f32[16,4736]{1,0:T(8,128)} collective-permute-done((f32[16,4736]{1,0:T(8,128)S(1)}, f32[16,4736]{1,0:T(8,128)}, u32[]{:S(2)}, u32[]{:S(2)}) %collective-permute-start.32) | collective-permute-done | bytes 303136 | tf_op jit(solution)/shard_map/ppermute | solution.py:152
  474.2 3.7 write_flat.7
  477.9 9.5 %collective-permute-start.41 = (f32[16,4736]{1,0:T(8,128)}, f32[16,4736]{1,0:T(8,128)S(1)}, u32[]{:S(2)}, u32[]{:S(2)}) collective-permute-start(f32[16,4736]{1,0:T(8,128)} %get-tuple-element.138), channel_id=1, source_target_pairs={{0,2},{1,3},{2,0},{3,1},{4,6},{5,7},{6,4},{7,5},{8,10},{9,11},{10,... | collective-permute-start | bytes 909320 | tf_op jit(solution)/shard_map/ppermute | solution.py:152
  488.7 2.7 fusion.68
  492.4 3.5 collective-permute-start.36
  495.8 22.4 %collective-permute-done.41.refs_2_ = f32[16,4736]{1,0:T(8,128)S(1)} collective-permute-done((f32[16,4736]{1,0:T(8,128)}, f32[16,4736]{1,0:T(8,128)S(1)}, u32[]{:S(2)}, u32[]{:S(2)}) %collective-permute-start.41) | collective-permute-done | bytes 303136 | tf_op jit(solution)/shard_map/ppermute | solution.py:152
  519.8 3.5 write_flat.8
  523.3 1.5 collective-permute-done.37.refs_2_
  524.8 5.7 %collective-permute-done.38.refs_3_ = f32[16,4736]{1,0:T(8,128)S(1)} collective-permute-done((f32[16,4736]{1,0:T(8,128)S(1)}, f32[16,4736]{1,0:T(8,128)S(1)}, u32[]{:S(2)}, u32[]{:S(2)}) %collective-permute-start.38) | collective-permute-done | bytes 303136 | tf_op jit(solution)/shard_map/ppermute | solution.py:152
  531.3 3.5 write_flat.9
  (169 shorter events, 45.5 us)
Async XLA Ops:
  0.8 21.5 %slice-start = ((s8[9699328]{0:T(1024)(128)(4,1)}), s8[4194304]{0:T(1024)(128)(4,1)S(1)}, s32[]{:S(2)}) async-start(s8[9699328]{0:T(1024)(128)(4,1)} %bitcast.564), calls=%async_computation | async-start | bytes 8388608
  9.8 12.5 %slice-start.1 = ((s8[9699328]{0:T(1024)(128)(4,1)}), s8[4194304]{0:T(1024)(128)(4,1)S(1)}, s32[]{:S(2)}) async-start(s8[9699328]{0:T(1024)(128)(4,1)} %bitcast.564), calls=%async_computation.1 | async-start | bytes 8388608
  9.8 12.5 %slice-start.2 = ((s8[9699328]{0:T(1024)(128)(4,1)}), s8[1310720]{0:T(1024)(128)(4,1)S(1)}, s32[]{:S(2)}) async-start(s8[9699328]{0:T(1024)(128)(4,1)} %bitcast.564), calls=%async_computation.2 | async-start | bytes 2621440
  21.8 25.6 %collective-permute-start = (f32[512,4736]{1,0:T(8,128)}, f32[512,4736]{1,0:T(8,128)}, u32[]{:S(2)}, u32[]{:S(2)}) collective-permute-start(f32[512,4736]{1,0:T(8,128)} %fusion.113), channel_id=1, source_target_pairs={{0,4},{4,0},{8,12},{12,8},{16,20},{20,16},{24,28},{28,24},{1,5},{5... | collective-permute-start | bytes 29097992 | tf_op jit(solution)/shard_map/ppermute | solution.py:155
  30.1 40.7 %collective-permute-start.1 = (f32[512,4736]{1,0:T(8,128)}, f32[512,4736]{1,0:T(8,128)}, u32[]{:S(2)}, u32[]{:S(2)}) collective-permute-start(f32[512,4736]{1,0:T(8,128)} %fusion.114), channel_id=1, source_target_pairs={{0,4},{4,0},{8,12},{12,8},{16,20},{20,16},{24,28},{28,24},{1,5},{5... | collective-permute-start | bytes 29097992 | tf_op jit(solution)/shard_map/ppermute | solution.py:155
  36.3 310.5 %collective-permute-start.20 = (f32[112,4736]{1,0:T(8,128)}, f32[112,4736]{1,0:T(8,128)}, u32[]{:S(2)}, u32[]{:S(2)}) collective-permute-start(f32[112,4736]{1,0:T(8,128)} %dynamic-slice_bitcast_fusion.1), channel_id=1, source_target_pairs={{0,2},{1,3},{2,0},{3,1},{4,6},{5,7},{6,4},{7,5},{8,10},{9,11},{10,... | collective-permute-start | bytes 6365192 | tf_op jit(solution)/shard_map/ppermute | solution.py:152
  44.1 21.0 %slice-start.3 = ((s8[9699328]{0:T(1024)(128)(4,1)}), s8[4194304]{0:T(1024)(128)(4,1)S(1)}, s32[]{:S(2)}) async-start(s8[9699328]{0:T(1024)(128)(4,1)} %bitcast.566), calls=%async_computation.3 | async-start | bytes 8388608
  47.3 17.8 %slice-start.4 = ((s8[9699328]{0:T(1024)(128)(4,1)}), s8[4194304]{0:T(1024)(128)(4,1)S(1)}, s32[]{:S(2)}) async-start(s8[9699328]{0:T(1024)(128)(4,1)} %bitcast.566), calls=%async_computation.4 | async-start | bytes 8388608
  47.3 17.8 %slice-start.5 = ((s8[9699328]{0:T(1024)(128)(4,1)}), s8[1310720]{0:T(1024)(128)(4,1)S(1)}, s32[]{:S(2)}) async-start(s8[9699328]{0:T(1024)(128)(4,1)} %bitcast.566), calls=%async_computation.5 | async-start | bytes 2621440
  59.9 54.6 %collective-permute-start.2 = (f32[2,2,32,4736]{3,2,1,0:T(8,128)}, f32[2,2,32,4736]{3,2,1,0:T(8,128)}, u32[]{:S(2)}, u32[]{:S(2)}) collective-permute-start(f32[2,2,32,4736]{3,2,1,0:T(8,128)} %slice_bitcast_fusion.2), channel_id=1, source_target_pairs={{0,8},{4,12},{8,0},{12,4},{16,24},{20,28},{24,16},{28,20},{1,9},{5... | collective-permute-start | bytes 7274504 | tf_op jit(solution)/shard_map/ppermute | solution.py:155
  63.6 55.8 %collective-permute-start.3 = (f32[2,2,32,4736]{3,2,1,0:T(8,128)}, f32[2,2,32,4736]{3,2,1,0:T(8,128)}, u32[]{:S(2)}, u32[]{:S(2)}) collective-permute-start(f32[2,2,32,4736]{3,2,1,0:T(8,128)} %slice_bitcast_fusion.3), channel_id=1, source_target_pairs={{0,16},{4,20},{8,24},{12,28},{16,0},{20,4},{24,8},{28,12},{1,17},{... | collective-permute-start | bytes 7274504 | tf_op jit(solution)/shard_map/ppermute | solution.py:155
  69.6 56.7 %collective-permute-start.4 = (f32[256,4736]{1,0:T(8,128)}, f32[256,4736]{1,0:T(8,128)}, u32[]{:S(2)}, u32[]{:S(2)}) collective-permute-start(f32[256,4736]{1,0:T(8,128)} %fusion.115), channel_id=1, source_target_pairs={{0,4},{4,0},{8,12},{12,8},{16,20},{20,16},{24,28},{28,24},{1,5},{5... | collective-permute-start | bytes 14549000 | tf_op jit(solution)/shard_map/ppermute | solution.py:155
  80.9 35.1 %copy-start.10 = (f32[2,32,4736]{2,1,0:T(8,128)S(1)}, f32[2,32,4736]{2,1,0:T(8,128)}, u32[]{:S(2)}) copy-start(f32[2,32,4736]{2,1,0:T(8,128)} %get-tuple-element.78) | copy-start | bytes 3637252
  82.5 90.4 %collective-permute-start.6 = (f32[2,2,32,4736]{3,2,1,0:T(8,128)}, f32[2,2,32,4736]{3,2,1,0:T(8,128)}, u32[]{:S(2)}, u32[]{:S(2)}) collective-permute-start(f32[2,2,32,4736]{3,2,1,0:T(8,128)} %slice_bitcast_fusion.1), channel_id=1, source_target_pairs={{0,16},{4,20},{8,24},{12,28},{16,0},{20,4},{24,8},{28,12},{1,17},{... | collective-permute-start | bytes 7274504 | tf_op jit(solution)/shard_map/ppermute | solution.py:155
  83.2 38.7 %copy-start.1 = (bf16[256,1024]{1,0:T(8,128)(2,1)S(1)}, bf16[256,1024]{1,0:T(8,128)(2,1)}, u32[]{:S(2)}) copy-start(bf16[256,1024]{1,0:T(8,128)(2,1)} %copy-done) | copy-start | bytes 1572868
  114.5 55.8 %collective-permute-start.5 = (f32[2,2,32,4736]{3,2,1,0:T(8,128)}, f32[2,2,32,4736]{3,2,1,0:T(8,128)}, u32[]{:S(2)}, u32[]{:S(2)}) collective-permute-start(f32[2,2,32,4736]{3,2,1,0:T(8,128)} %slice_bitcast_fusion), channel_id=1, source_target_pairs={{0,8},{4,12},{8,0},{12,4},{16,24},{20,28},{24,16},{28,20},{1,9},{5... | collective-permute-start | bytes 7274504 | tf_op jit(solution)/shard_map/ppermute | solution.py:155
  121.8 74.4 %collective-permute-start.7 = (f32[2,32,4736]{2,1,0:T(8,128)}, f32[2,32,4736]{2,1,0:T(8,128)S(1)}, u32[]{:S(2)}, u32[]{:S(2)}) collective-permute-start(f32[2,32,4736]{2,1,0:T(8,128)} %fusion.2), channel_id=1, source_target_pairs={{0,8},{4,12},{8,0},{12,4},{16,24},{20,28},{24,16},{28,20},{1,9},{5... | collective-permute-start | bytes 3637256 | tf_op jit(solution)/shard_map/ppermute | solution.py:155
  126.3 71.5 %collective-permute-start.15 = (f32[2,32,4736]{2,1,0:T(8,128)}, f32[2,32,4736]{2,1,0:T(8,128)S(1)}, u32[]{:S(2)}, u32[]{:S(2)}) collective-permute-start(f32[2,32,4736]{2,1,0:T(8,128)} %fusion.3), channel_id=1, source_target_pairs={{0,16},{4,20},{8,24},{12,28},{16,0},{20,4},{24,8},{28,12},{1,17},{... | collective-permute-start | bytes 3637256 | tf_op jit(solution)/shard_map/ppermute | solution.py:155
  132.8 75.2 %copy-start.9 = (f32[256,4736]{1,0:T(8,128)}, f32[256,4736]{1,0:T(8,128)S(1)}, u32[]{:S(2)}) copy-start(f32[256,4736]{1,0:T(8,128)S(1)} %convolution_add_fusion.4) | copy-start | bytes 14548996
  170.3 37.7 %collective-permute-start.8 = (f32[256,4736]{1,0:T(8,128)}, f32[256,4736]{1,0:T(8,128)}, u32[]{:S(2)}, u32[]{:S(2)}) collective-permute-start(f32[256,4736]{1,0:T(8,128)} %fusion.116), channel_id=1, source_target_pairs={{0,4},{4,0},{8,12},{12,8},{16,20},{20,16},{24,28},{28,24},{1,5},{5... | collective-permute-start | bytes 14549000 | tf_op jit(solution)/shard_map/ppermute | solution.py:155
  175.4 81.2 %collective-permute-start.11 = (f32[2,32,4736]{2,1,0:T(8,128)}, f32[2,32,4736]{2,1,0:T(8,128)}, u32[]{:S(2)}, u32[]{:S(2)}) collective-permute-start(f32[2,32,4736]{2,1,0:T(8,128)} %fusion), channel_id=1, source_target_pairs={{0,8},{4,12},{8,0},{12,4},{16,24},{20,28},{24,16},{28,20},{1,9},{5... | collective-permute-start | bytes 3637256 | tf_op jit(solution)/shard_map/ppermute | solution.py:155
  196.2 53.5 %collective-permute-start.10 = (f32[2,2,16,4736]{3,2,1,0:T(8,128)}, f32[2,2,16,4736]{3,2,1,0:T(8,128)}, u32[]{:S(2)}, u32[]{:S(2)}) collective-permute-start(f32[2,2,16,4736]{3,2,1,0:T(8,128)} %slice_bitcast_fusion.11), channel_id=1, source_target_pairs={{0,16},{4,20},{8,24},{12,28},{16,0},{20,4},{24,8},{28,12},{1,17},{... | collective-permute-start | bytes 3637256 | tf_op jit(solution)/shard_map/ppermute | solution.py:155
  197.7 48.5 %collective-permute-start.9 = (f32[2,2,16,4736]{3,2,1,0:T(8,128)}, f32[2,2,16,4736]{3,2,1,0:T(8,128)}, u32[]{:S(2)}, u32[]{:S(2)}) collective-permute-start(f32[2,2,16,4736]{3,2,1,0:T(8,128)} %slice_bitcast_fusion.10), channel_id=1, source_target_pairs={{0,8},{4,12},{8,0},{12,4},{16,24},{20,28},{24,16},{28,20},{1,9},{5... | collective-permute-start | bytes 3637256 | tf_op jit(solution)/shard_map/ppermute | solution.py:155
  208.0 71.2 %collective-permute-start.12 = (f32[256,4736]{1,0:T(8,128)}, f32[256,4736]{1,0:T(8,128)}, u32[]{:S(2)}, u32[]{:S(2)}) collective-permute-start(f32[256,4736]{1,0:T(8,128)} %fusion.117), channel_id=1, source_target_pairs={{0,4},{4,0},{8,12},{12,8},{16,20},{20,16},{24,28},{28,24},{1,5},{5... | collective-permute-start | bytes 14549000 | tf_op jit(solution)/shard_map/ppermute | solution.py:155
  213.1 66.1 %copy-start.7 = (f32[256,4736]{1,0:T(8,128)}, f32[256,4736]{1,0:T(8,128)S(1)}, u32[]{:S(2)}) copy-start(f32[256,4736]{1,0:T(8,128)S(1)} %convolution_add_fusion.3) | copy-start | bytes 14548996
  213.1 33.1 %copy-start.11 = (f32[2,32,4736]{2,1,0:T(8,128)S(1)}, f32[2,32,4736]{2,1,0:T(8,128)}, u32[]{:S(2)}) copy-start(f32[2,32,4736]{2,1,0:T(8,128)} %fusion.1) | copy-start | bytes 3637252
  246.2 26.7 %collective-permute-start.25 = (f32[2,32,4736]{2,1,0:T(8,128)S(1)}, f32[2,32,4736]{2,1,0:T(8,128)}, u32[]{:S(2)}, u32[]{:S(2)}) collective-permute-start(f32[2,32,4736]{2,1,0:T(8,128)S(1)} %copy-done.11), channel_id=1, source_target_pairs={{0,16},{4,20},{8,24},{12,28},{16,0},{20,4},{24,8},{28,12},{1,17},{... | collective-permute-start | bytes 3637256 | tf_op jit(solution)/shard_map/ppermute | solution.py:155
  249.7 98.8 %collective-permute-start.19 = (f32[112,4736]{1,0:T(8,128)}, f32[112,4736]{1,0:T(8,128)S(1)}, u32[]{:S(2)}, u32[]{:S(2)}) collective-permute-start(f32[112,4736]{1,0:T(8,128)} %dynamic-slice_bitcast_fusion.2), channel_id=1, source_target_pairs={{0,1},{1,2},{2,3},{3,0},{4,5},{5,6},{6,7},{7,4},{8,9},{9,10},{10,1... | collective-permute-start | bytes 6365192 | tf_op jit(solution)/shard_map/ppermute | solution.py:152
  256.6 87.1 %collective-permute-start.21 = (f32[112,4736]{1,0:T(8,128)}, f32[112,4736]{1,0:T(8,128)S(1)}, u32[]{:S(2)}, u32[]{:S(2)}) collective-permute-start(f32[112,4736]{1,0:T(8,128)} %dynamic-slice_bitcast_fusion), channel_id=1, source_target_pairs={{0,3},{1,0},{2,1},{3,2},{4,7},{5,4},{6,5},{7,6},{8,11},{9,8},{10,9... | collective-permute-start | bytes 6365192 | tf_op jit(solution)/shard_map/ppermute | solution.py:152
  273.0 77.1 %collective-permute-start.14 = (f32[2,2,16,4736]{3,2,1,0:T(8,128)}, f32[2,2,16,4736]{3,2,1,0:T(8,128)S(1)}, u32[]{:S(2)}, u32[]{:S(2)}) collective-permute-start(f32[2,2,16,4736]{3,2,1,0:T(8,128)} %slice_bitcast_fusion.7), channel_id=1, source_target_pairs={{0,16},{4,20},{8,24},{12,28},{16,0},{20,4},{24,8},{28,12},{1,17},{... | collective-permute-start | bytes 3637256 | tf_op jit(solution)/shard_map/ppermute | solution.py:155
  279.3 25.8 %collective-permute-start.13 = (f32[2,2,16,4736]{3,2,1,0:T(8,128)}, f32[2,2,16,4736]{3,2,1,0:T(8,128)S(1)}, u32[]{:S(2)}, u32[]{:S(2)}) collective-permute-start(f32[2,2,16,4736]{3,2,1,0:T(8,128)} %slice_bitcast_fusion.6), channel_id=1, source_target_pairs={{0,8},{4,12},{8,0},{12,4},{16,24},{20,28},{24,16},{28,20},{1,9},{5... | collective-permute-start | bytes 3637256 | tf_op jit(solution)/shard_map/ppermute | solution.py:155
  285.8 64.2 %copy-start.8 = (f32[256,4736]{1,0:T(8,128)}, f32[256,4736]{1,0:T(8,128)S(1)}, u32[]{:S(2)}) copy-start(f32[256,4736]{1,0:T(8,128)S(1)} %convolution_add_fusion.2) | copy-start | bytes 14548996
  285.8 19.2 %copy-start.21 = (f32[32,4736]{1,0:T(8,128)S(1)}, f32[32,4736]{1,0:T(8,128)}, u32[]{:S(2)}) copy-start(f32[32,4736]{1,0:T(8,128)} %get-tuple-element.127) | copy-start | bytes 1818628
  285.9 57.8 %copy-start.23 = (f32[32,4736]{1,0:T(8,128)S(1)}, f32[32,4736]{1,0:T(8,128)}, u32[]{:S(2)}) copy-start(f32[32,4736]{1,0:T(8,128)} %get-tuple-element.126) | copy-start | bytes 1818628
  285.9 61.0 %copy-start.22 = (f32[32,4736]{1,0:T(8,128)S(1)}, f32[32,4736]{1,0:T(8,128)}, u32[]{:S(2)}) copy-start(f32[32,4736]{1,0:T(8,128)} %get-tuple-element.133) | copy-start | bytes 1818628
  305.1 90.0 %copy-start.14 = (f32[2,2,16,4736]{3,2,1,0:T(8,128)}, f32[2,2,16,4736]{3,2,1,0:T(8,128)S(1)}, u32[]{:S(2)}) copy-start(f32[2,2,16,4736]{3,2,1,0:T(8,128)S(1)} %collective-permute-done.13) | copy-start | bytes 3637252
  305.1 90.7 %collective-permute-start.18 = (f32[32,4736]{1,0:T(8,128)S(1)}, f32[32,4736]{1,0:T(8,128)S(1)}, u32[]{:S(2)}, u32[]{:S(2)}) collective-permute-start(f32[32,4736]{1,0:T(8,128)S(1)} %copy-done.21), channel_id=1, source_target_pairs={{0,3},{1,0},{2,1},{3,2},{4,7},{5,4},{6,5},{7,6},{8,11},{9,8},{10,9... | collective-permute-start | bytes 1818632 | tf_op jit(solution)/shard_map/ppermute | solution.py:152
  343.7 51.4 %collective-permute-start.17 = (f32[32,4736]{1,0:T(8,128)S(1)}, f32[32,4736]{1,0:T(8,128)S(1)}, u32[]{:S(2)}, u32[]{:S(2)}) collective-permute-start(f32[32,4736]{1,0:T(8,128)S(1)} %copy-done.23), channel_id=1, source_target_pairs={{0,2},{1,3},{2,0},{3,1},{4,6},{5,7},{6,4},{7,5},{8,10},{9,11},{10,... | collective-permute-start | bytes 1818632 | tf_op jit(solution)/shard_map/ppermute | solution.py:152
  346.9 48.2 %collective-permute-start.16 = (f32[32,4736]{1,0:T(8,128)S(1)}, f32[32,4736]{1,0:T(8,128)S(1)}, u32[]{:S(2)}, u32[]{:S(2)}) collective-permute-start(f32[32,4736]{1,0:T(8,128)S(1)} %copy-done.22), channel_id=1, source_target_pairs={{0,1},{1,2},{2,3},{3,0},{4,5},{5,6},{6,7},{7,4},{8,9},{9,10},{10,1... | collective-permute-start | bytes 1818632 | tf_op jit(solution)/shard_map/ppermute | solution.py:152
  348.5 49.4 %copy-start.4 = (f32[112,4736]{1,0:T(8,128)}, f32[112,4736]{1,0:T(8,128)S(1)}, u32[]{:S(2)}) copy-start(f32[112,4736]{1,0:T(8,128)S(1)} %collective-permute-done.19.refs_5_) | copy-start | bytes 6365188
  348.5 56.6 %collective-permute-start.22 = (f32[2,16,4736]{2,1,0:T(8,128)}, f32[2,16,4736]{2,1,0:T(8,128)}, u32[]{:S(2)}, u32[]{:S(2)}) collective-permute-start(f32[2,16,4736]{2,1,0:T(8,128)} %fusion.43), channel_id=1, source_target_pairs={{0,8},{4,12},{8,0},{12,4},{16,24},{20,28},{24,16},{28,20},{1,9},{5... | collective-permute-start | bytes 1818632 | tf_op jit(solution)/shard_map/ppermute | solution.py:155
  350.1 55.6 %collective-permute-start.30 = (f32[2,16,4736]{2,1,0:T(8,128)}, f32[2,16,4736]{2,1,0:T(8,128)}, u32[]{:S(2)}, u32[]{:S(2)}) collective-permute-start(f32[2,16,4736]{2,1,0:T(8,128)} %fusion.44), channel_id=1, source_target_pairs={{0,16},{4,20},{8,24},{12,28},{16,0},{20,4},{24,8},{28,12},{1,17},{... | collective-permute-start | bytes 1818632 | tf_op jit(solution)/shard_map/ppermute | solution.py:155
  395.0 55.9 %collective-permute-start.28 = (f32[32,4736]{1,0:T(8,128)S(1)}, f32[32,4736]{1,0:T(8,128)}, u32[]{:S(2)}, u32[]{:S(2)}) collective-permute-start(f32[32,4736]{1,0:T(8,128)S(1)} %get-tuple-element.123), channel_id=1, source_target_pairs={{0,3},{1,0},{2,1},{3,2},{4,7},{5,4},{6,5},{7,6},{8,11},{9,8},{10,9... | collective-permute-start | bytes 1818632 | tf_op jit(solution)/shard_map/ppermute | solution.py:152
  395.0 52.5 %collective-permute-start.27 = (f32[32,4736]{1,0:T(8,128)}, f32[32,4736]{1,0:T(8,128)}, u32[]{:S(2)}, u32[]{:S(2)}) collective-permute-start(f32[32,4736]{1,0:T(8,128)} %get-tuple-element.122), channel_id=1, source_target_pairs={{0,2},{1,3},{2,0},{3,1},{4,6},{5,7},{6,4},{7,5},{8,10},{9,11},{10,... | collective-permute-start | bytes 1818632 | tf_op jit(solution)/shard_map/ppermute | solution.py:152
  396.6 50.9 %collective-permute-start.26 = (f32[32,4736]{1,0:T(8,128)}, f32[32,4736]{1,0:T(8,128)}, u32[]{:S(2)}, u32[]{:S(2)}) collective-permute-start(f32[32,4736]{1,0:T(8,128)} %get-tuple-element.131), channel_id=1, source_target_pairs={{0,1},{1,2},{2,3},{3,0},{4,5},{5,6},{6,7},{7,4},{8,9},{9,10},{10,1... | collective-permute-start | bytes 1818632 | tf_op jit(solution)/shard_map/ppermute | solution.py:152
  405.1 31.0 %collective-permute-start.24 = (f32[2,2,16,4736]{3,2,1,0:T(8,128)}, f32[2,2,16,4736]{3,2,1,0:T(8,128)S(1)}, u32[]{:S(2)}, u32[]{:S(2)}) collective-permute-start(f32[2,2,16,4736]{3,2,1,0:T(8,128)} %slice_bitcast_fusion.5), channel_id=1, source_target_pairs={{0,16},{4,20},{8,24},{12,28},{16,0},{20,4},{24,8},{28,12},{1,17},{... | collective-permute-start | bytes 3637256 | tf_op jit(solution)/shard_map/ppermute | solution.py:155
  405.7 28.0 %collective-permute-start.23 = (f32[2,2,16,4736]{3,2,1,0:T(8,128)}, f32[2,2,16,4736]{3,2,1,0:T(8,128)S(1)}, u32[]{:S(2)}, u32[]{:S(2)}) collective-permute-start(f32[2,2,16,4736]{3,2,1,0:T(8,128)} %slice_bitcast_fusion.4), channel_id=1, source_target_pairs={{0,8},{4,12},{8,0},{12,4},{16,24},{20,28},{24,16},{28,20},{1,9},{5... | collective-permute-start | bytes 3637256 | tf_op jit(solution)/shard_map/ppermute | solution.py:155
  433.6 17.3 %copy-start.18 = (f32[2,2,16,4736]{3,2,1,0:T(8,128)}, f32[2,2,16,4736]{3,2,1,0:T(8,128)S(1)}, u32[]{:S(2)}) copy-start(f32[2,2,16,4736]{3,2,1,0:T(8,128)S(1)} %collective-permute-done.23) | copy-start | bytes 3637252
  433.6 24.7 %collective-permute-start.29 = (f32[2,16,4736]{2,1,0:T(8,128)}, f32[2,16,4736]{2,1,0:T(8,128)}, u32[]{:S(2)}, u32[]{:S(2)}) collective-permute-start(f32[2,16,4736]{2,1,0:T(8,128)} %fusion.36), channel_id=1, source_target_pairs={{0,8},{4,12},{8,0},{12,4},{16,24},{20,28},{24,16},{28,20},{1,9},{5... | collective-permute-start | bytes 1818632 | tf_op jit(solution)/shard_map/ppermute | solution.py:155
  436.0 14.9 %copy-start.16 = (f32[2,2,16,4736]{3,2,1,0:T(8,128)}, f32[2,2,16,4736]{3,2,1,0:T(8,128)S(1)}, u32[]{:S(2)}) copy-start(f32[2,2,16,4736]{3,2,1,0:T(8,128)S(1)} %collective-permute-done.24) | copy-start | bytes 3637252
  436.1 23.8 %collective-permute-start.39 = (f32[2,16,4736]{2,1,0:T(8,128)}, f32[2,16,4736]{2,1,0:T(8,128)}, u32[]{:S(2)}, u32[]{:S(2)}) collective-permute-start(f32[2,16,4736]{2,1,0:T(8,128)} %fusion.37), channel_id=1, source_target_pairs={{0,16},{4,20},{8,24},{12,28},{16,0},{20,4},{24,8},{28,12},{1,17},{... | collective-permute-start | bytes 1818632 | tf_op jit(solution)/shard_map/ppermute | solution.py:155
  447.5 26.7 %collective-permute-start.33 = (f32[16,4736]{1,0:T(8,128)}, f32[16,4736]{1,0:T(8,128)}, u32[]{:S(2)}, u32[]{:S(2)}) collective-permute-start(f32[16,4736]{1,0:T(8,128)} %get-tuple-element.147), channel_id=1, source_target_pairs={{0,3},{1,0},{2,1},{3,2},{4,7},{5,4},{6,5},{7,6},{8,11},{9,8},{10,9... | collective-permute-start | bytes 909320 | tf_op jit(solution)/shard_map/ppermute | solution.py:152
  447.5 26.7 %collective-permute-start.32 = (f32[16,4736]{1,0:T(8,128)S(1)}, f32[16,4736]{1,0:T(8,128)}, u32[]{:S(2)}, u32[]{:S(2)}) collective-permute-start(f32[16,4736]{1,0:T(8,128)S(1)} %get-tuple-element.146), channel_id=1, source_target_pairs={{0,2},{1,3},{2,0},{3,1},{4,6},{5,7},{6,4},{7,5},{8,10},{9,11},{10,... | collective-permute-start | bytes 909320 | tf_op jit(solution)/shard_map/ppermute | solution.py:152
  450.9 23.2 %collective-permute-start.31 = (f32[16,4736]{1,0:T(8,128)}, f32[16,4736]{1,0:T(8,128)}, u32[]{:S(2)}, u32[]{:S(2)}) collective-permute-start(f32[16,4736]{1,0:T(8,128)} %get-tuple-element.155), channel_id=1, source_target_pairs={{0,1},{1,2},{2,3},{3,0},{4,5},{5,6},{6,7},{7,4},{8,9},{9,10},{10,1... | collective-permute-start | bytes 909320 | tf_op jit(solution)/shard_map/ppermute | solution.py:152
  458.3 30.4 %collective-permute-start.34 = (f32[2,16,4736]{2,1,0:T(8,128)}, f32[2,16,4736]{2,1,0:T(8,128)}, u32[]{:S(2)}, u32[]{:S(2)}) collective-permute-start(f32[2,16,4736]{2,1,0:T(8,128)} %fusion.19), channel_id=1, source_target_pairs={{0,8},{4,12},{8,0},{12,4},{16,24},{20,28},{24,16},{28,20},{1,9},{5... | collective-permute-start | bytes 1818632 | tf_op jit(solution)/shard_map/ppermute | solution.py:155
  459.9 28.8 %collective-permute-start.35 = (f32[2,16,4736]{2,1,0:T(8,128)S(1)}, f32[2,16,4736]{2,1,0:T(8,128)}, u32[]{:S(2)}, u32[]{:S(2)}) collective-permute-start(f32[2,16,4736]{2,1,0:T(8,128)S(1)} %copy-done.24), channel_id=1, source_target_pairs={{0,16},{4,20},{8,24},{12,28},{16,0},{20,4},{24,8},{28,12},{1,17},{... | collective-permute-start | bytes 1818632 | tf_op jit(solution)/shard_map/ppermute | solution.py:155
  474.2 44.2 %collective-permute-start.42 = (f32[16,4736]{1,0:T(8,128)}, f32[16,4736]{1,0:T(8,128)S(1)}, u32[]{:S(2)}, u32[]{:S(2)}) collective-permute-start(f32[16,4736]{1,0:T(8,128)} %get-tuple-element.139), channel_id=1, source_target_pairs={{0,3},{1,0},{2,1},{3,2},{4,7},{5,4},{6,5},{7,6},{8,11},{9,8},{10,9... | collective-permute-start | bytes 909320 | tf_op jit(solution)/shard_map/ppermute | solution.py:152
  474.2 14.5 %copy-start.17 = (f32[2,2,16,4736]{3,2,1,0:T(8,128)S(1)}, f32[2,2,16,4736]{3,2,1,0:T(8,128)}, u32[]{:S(2)}) copy-start(f32[2,2,16,4736]{3,2,1,0:T(8,128)} %copy-done.16) | copy-start | bytes 3637252
  474.2 14.5 %copy-start.19 = (f32[2,2,16,4736]{3,2,1,0:T(8,128)S(1)}, f32[2,2,16,4736]{3,2,1,0:T(8,128)}, u32[]{:S(2)}) copy-start(f32[2,2,16,4736]{3,2,1,0:T(8,128)} %copy-done.18) | copy-start | bytes 3637252
  477.9 40.4 %collective-permute-start.41 = (f32[16,4736]{1,0:T(8,128)}, f32[16,4736]{1,0:T(8,128)S(1)}, u32[]{:S(2)}, u32[]{:S(2)}) collective-permute-start(f32[16,4736]{1,0:T(8,128)} %get-tuple-element.138), channel_id=1, source_target_pairs={{0,2},{1,3},{2,0},{3,1},{4,6},{5,7},{6,4},{7,5},{8,10},{9,11},{10,... | collective-permute-start | bytes 909320 | tf_op jit(solution)/shard_map/ppermute | solution.py:152
  487.3 31.0 %collective-permute-start.40 = (f32[16,4736]{1,0:T(8,128)}, f32[16,4736]{1,0:T(8,128)S(1)}, u32[]{:S(2)}, u32[]{:S(2)}) collective-permute-start(f32[16,4736]{1,0:T(8,128)} %get-tuple-element.151), channel_id=1, source_target_pairs={{0,1},{1,2},{2,3},{3,0},{4,5},{5,6},{6,7},{7,4},{8,9},{9,10},{10,1... | collective-permute-start | bytes 909320 | tf_op jit(solution)/shard_map/ppermute | solution.py:152
  491.4 33.4 %collective-permute-start.37 = (f32[16,4736]{1,0:T(8,128)}, f32[16,4736]{1,0:T(8,128)S(1)}, u32[]{:S(2)}, u32[]{:S(2)}) collective-permute-start(f32[16,4736]{1,0:T(8,128)} %get-tuple-element.142), channel_id=1, source_target_pairs={{0,2},{1,3},{2,0},{3,1},{4,6},{5,7},{6,4},{7,5},{8,10},{9,11},{10,... | collective-permute-start | bytes 909320 | tf_op jit(solution)/shard_map/ppermute | solution.py:152
  492.4 32.5 %collective-permute-start.36 = (f32[16,4736]{1,0:T(8,128)S(1)}, f32[16,4736]{1,0:T(8,128)S(1)}, u32[]{:S(2)}, u32[]{:S(2)}) collective-permute-start(f32[16,4736]{1,0:T(8,128)S(1)} %get-tuple-element.153), channel_id=1, source_target_pairs={{0,1},{1,2},{2,3},{3,0},{4,5},{5,6},{6,7},{7,4},{8,9},{9,10},{10,1... | collective-permute-start | bytes 909320 | tf_op jit(solution)/shard_map/ppermute | solution.py:152
  518.3 12.2 %collective-permute-start.38 = (f32[16,4736]{1,0:T(8,128)S(1)}, f32[16,4736]{1,0:T(8,128)S(1)}, u32[]{:S(2)}, u32[]{:S(2)}) collective-permute-start(f32[16,4736]{1,0:T(8,128)S(1)} %get-tuple-element.143), channel_id=1, source_target_pairs={{0,3},{1,0},{2,1},{3,2},{4,7},{5,4},{6,5},{7,6},{8,11},{9,8},{10,9... | collective-permute-start | bytes 909320 | tf_op jit(solution)/shard_map/ppermute | solution.py:152
  (21 other events, 122.2 us)
